TPU v7x, 256 devices: a whole 4x4x8 slice. The times are simulated.
256 devices in a mesh: dp: 8 (over y, core), head: 2 (over z_lo), kv: 16 (over z_hi, x).
Axes of the slice: x: 4, y: 4, z: 8 (z_hi: 4, z_lo: 2; z = z_hi * 2 + z_lo), core: 2. Of those that a mesh axis runs over, the one named last changes fastest.
Arguments:
- teacher_query: bfloat16 [8, 4096, 3584], P('dp', 'kv', 'head'), may hold values from -96 to 96
- teacher_key: bfloat16 [8, 4096, 512], P('dp', 'kv', 'head'), may hold values from -8 to 8
- student_query: bfloat16 [8, 4096, 1792], P('dp', 'kv', 'head'), may hold values from -96 to 96
- student_key: bfloat16 [8, 4096, 256], P('dp', 'kv', 'head'), may hold values from -8 to 8
- pair_table: int32 [14, 2], replicated, may hold values from 0 to 27, as said below
Outputs:
- kl: float32 [8, 14, 4096], P('dp', 'head', 'kv')
- head_loss: float32 [14], P('head')
Inputs may be any that keep to these rules, and one draw needn't show every extreme that they name: `pair_table`: each of the 28 teacher heads appears exactly once in the table.
All inputs are finite; a program needn't handle non-finite values.
Results may differ from a plain program's by a relative error of at most 0.0003.
Values may be sent and summed in bfloat16 or wider, within the bound.
No kernel may reach another device: no remote copies, remote signals or barrier semaphores. Data moves between devices by JAX's collectives and lax.ppermute only.
A program may use at most 64 MiB of HBM per device.

v0:
```python
import math
import jax
import jax.numpy as jnp
from jax import lax
from jax.sharding import Mesh
from jax.sharding import PartitionSpec as P

HT = 28
KVT = 4
DH = 128
HS = 14
KVS = 2
KV = ("kv_0", "kv_1")
DP = ("dp_0", "dp_1")
DP_KV = ("dp_0", "dp_1", "kv_0", "kv_1")
masked_value = -1e30


def from_everyone(shard, axis):
    count = lax.axis_size(axis)
    return lax.all_to_all(
        jnp.broadcast_to(shard[None], (count, *shard.shape)), axis, 0, 0, tiled=True
    )


def joined_along(blocks, dim):
    dims = list(blocks.shape[1:])
    dims[dim] *= blocks.shape[0]
    return jnp.moveaxis(blocks, 0, dim).reshape(dims)


def gathered_copies(shard, axis, dim):
    blocks = from_everyone(shard, axis)
    return joined_along(blocks, dim)


def one_axis_at_a_time(shard, axes):
    for axis in axes:
        shard = lax.psum(shard, axis)
    return shard


def running_softmax(running_max, running_total, logits, causal_mask):
    filled = jnp.where(causal_mask, logits, masked_value)
    new_max = jnp.maximum(running_max, jnp.max(filled, axis=-1))
    rescale = jnp.exp(running_max - new_max)
    weights = jnp.where(causal_mask, jnp.exp(filled - new_max[..., None]), 0.0)
    return (new_max, running_total * rescale + jnp.sum(weights, axis=-1), rescale, weights)


def make_fold(teacher_heads, teacher_select, student_heads, student_select, repeat, query_pos):
    seq_dev, row_count, pair_count, head_dim = teacher_heads.shape
    student_count = student_heads.shape[2]
    scale = 1.0 / math.sqrt(head_dim)
    last_query = query_pos[row_count - 1]

    def fold_step(carry, pieces, start):
        teacher_keys, student_keys = pieces
        key_count = teacher_keys.shape[1]
        block_size = math.gcd(key_count, 512)
        block_total = key_count // block_size
        visible = jnp.clip(last_query // block_size + 1, 0, block_total)

        def one_block(block_index, state):
            t_max, t_total, t_cross, s_max, s_total = state
            offset = block_index * block_size
            t_block = lax.dynamic_slice_in_dim(teacher_keys, offset, block_size, 1).reshape(
                seq_dev, block_size, -1, head_dim
            )
            s_block = lax.dynamic_slice_in_dim(student_keys, offset, block_size, 1).reshape(
                seq_dev, block_size, -1, head_dim
            )
            t_keys = jnp.take(t_block, teacher_select, axis=2)
            s_keys = jnp.take(s_block, student_select, axis=2)
            t_logits = (
                jnp.einsum(
                    "bqpd,bkpd->bpqk", teacher_heads, t_keys, preferred_element_type=jnp.float32
                )
                * scale
            )
            s_logits = (
                jnp.einsum(
                    "bqsd,bksd->bsqk", student_heads, s_keys, preferred_element_type=jnp.float32
                )
                * scale
            )
            key_pos = offset + jnp.arange(block_size, dtype=jnp.int32)
            causal_mask = key_pos[None, :] <= query_pos[:, None]
            t_max, t_total, t_rescale, t_weights = running_softmax(
                t_max, t_total, t_logits, causal_mask
            )
            s_max, s_total, s_rescale, s_weights = running_softmax(
                s_max, s_total, s_logits, causal_mask
            )
            split_logits = t_logits.reshape(seq_dev, student_count, repeat, row_count, block_size)
            gap = (split_logits - s_logits[:, :, None]).reshape(
                seq_dev, pair_count, row_count, block_size
            )
            t_cross = t_cross * t_rescale + jnp.sum(t_weights * gap, axis=-1)
            return (t_max, t_total, t_cross, s_max, s_total)

        return lax.fori_loop(0, visible, one_block, carry)

    pair_shape = (seq_dev, pair_count, row_count)
    student_shape = (seq_dev, student_count, row_count)
    initial = (
        jnp.full(pair_shape, masked_value, jnp.float32),
        jnp.zeros(pair_shape, jnp.float32),
        jnp.zeros(pair_shape, jnp.float32),
        jnp.full(student_shape, masked_value, jnp.float32),
        jnp.zeros(student_shape, jnp.float32),
    )
    return (fold_step, initial)


def finish_pairs(state, repeat):
    t_max, t_total, t_cross, s_max, s_total = state
    seq_dev, pair_count, row_count = t_max.shape
    student_count = s_max.shape[1]
    t_lse = t_max + jnp.log(t_total)
    s_lse = s_max + jnp.log(s_total)
    s_paired = jnp.broadcast_to(
        s_lse[:, :, None], (seq_dev, student_count, repeat, row_count)
    ).reshape(seq_dev, pair_count, row_count)
    return t_cross / t_total - t_lse + s_paired


def per_device(teacher_query, teacher_key, student_query, student_key, pair_table):
    seq_dev, row_count, teacher_width = teacher_query.shape
    n_head = lax.axis_size("head")
    n_kv = lax.axis_size(KV)
    n_data = lax.axis_size(DP)
    head_index = lax.axis_index("head")
    kv_index = lax.axis_index(KV)
    group_teacher = HT // KVT
    group_student = HS // KVS
    local_student = HS // n_head
    local_student_kv = KVS // n_head
    query_pos = kv_index * row_count + jnp.arange(row_count, dtype=jnp.int32)
    all_tq, all_tk = (
        gathered_copies(teacher_query, "head", 2),
        gathered_copies(teacher_key, "head", 2),
    )
    my_pairs = lax.dynamic_slice_in_dim(
        pair_table, head_index * local_student, local_student, 0
    ).reshape(-1)
    teacher_heads = jnp.take(all_tq.reshape(seq_dev, row_count, HT, DH), my_pairs, axis=2)
    teacher_select = my_pairs // group_teacher
    student_heads = student_query.reshape(seq_dev, row_count, local_student, DH)
    student_ids = head_index * local_student + jnp.arange(local_student, dtype=jnp.int32)
    student_select = student_ids // group_student - head_index * local_student_kv
    fold_step, initial = make_fold(
        teacher_heads, teacher_select, student_heads, student_select, 2, query_pos
    )
    state = fold_step(
        initial,
        (
            lax.all_gather(all_tk, KV, axis=1, tiled=True),
            lax.all_gather(student_key, KV, axis=1, tiled=True),
        ),
        jnp.int32(0),
    )
    pair_kl = finish_pairs(state, 2)
    kl_local = jnp.sum(pair_kl.reshape(seq_dev, local_student, 2, row_count), axis=2)
    head_sums = jnp.sum(kl_local, axis=(0, 2))
    total = one_axis_at_a_time(head_sums, DP_KV)
    head_loss = total / (seq_dev * n_data * row_count * n_kv)
    return (kl_local, head_loss)


def solution(mesh):
    split = Mesh(
        mesh.devices.reshape(4, 2, mesh.shape["head"], 4, 4),
        ("dp_0", "dp_1", "head", "kv_0", "kv_1"),
    )
    in_specs = (P(DP, KV, "head"), P(DP, KV, "head"), P(DP, KV, "head"), P(DP, KV, "head"), P())
    out_specs = (P(DP, "head", KV), P("head"))
    return jax.shard_map(
        per_device, mesh=split, in_specs=in_specs, out_specs=out_specs, check_vma=False
    )
```

profile of v0, /device:TPU:0, one launch (start us, length us, event | category | flops | bytes accessed | tf_op | source)
XLA Modules:
  0.0 263.1 jit_solution(12517146968400585087)
XLA Ops:
  7.2 0.7 all-gather.5.cloned.1.call-update
  8.0 1.0 copy.25
  9.0 8.2 %all_to_all.10 = bf16[2,1,256,256]{2,3,1,0:T(8,128)(2,1)} all-to-all(bf16[2,1,256,256]{2,3,1,0:T(8,128)(2,1)S(1)} %broadcast_in_dim.98), channel_id=1, replica_groups=mesh['dp_0'=4,'dp_1'=2,'head'=2,'kv_0'=4,'kv_1'=4] {'head'}, dimensions={0} | all-to-all | bytes 524288 | tf_op jit(solution)/shard_map/all_to_all | solution.py:21
  17.3 1.5 copy.26
  18.7 1.4 broadcast_in_dim.101
  20.1 3.7 %all-to-all-start.1 = ((bf16[2,1,256,1792]{2,3,1,0:T(8,128)(2,1)}), bf16[2,1,256,1792]{2,3,1,0:T(8,128)(2,1)S(1)}, u32[]{:S(2)}, u32[]{:S(2)}) async-start(bf16[2,1,256,1792]{2,3,1,0:T(8,128)(2,1)} %broadcast_in_dim.101), calls=%async_computation.1 | async-start | bytes 3670016 | tf_op jit(solution)/shard_map/all_to_all | solution.py:21
  23.9 0.6 slice.3
  27.4 0.2 copy.30
  27.6 1.0 copy.31
  28.7 16.9 %all-to-all-done.1 = bf16[2,1,256,1792]{2,3,1,0:T(8,128)(2,1)S(1)} async-done(((bf16[2,1,256,1792]{2,3,1,0:T(8,128)(2,1)}), bf16[2,1,256,1792]{2,3,1,0:T(8,128)(2,1)S(1)}, u32[]{:S(2)}, u32[]{:S(2)}) %all-to-all-start.1) | async-done | bytes 1835040 | tf_op jit(solution)/shard_map/all_to_all | solution.py:21
  45.6 2.6 copy.29
  48.2 2.2 gather_fusion.1
  50.4 0.1 bitcast_select_fusion.1
  50.6 15.0 %all-gather.5.cloned.1.call-done = bf16[1,4096,128]{2,1,0:T(8,128)(2,1)} async-done(((bf16[1,256,128]{2,1,0:T(8,128)(2,1)}), bf16[1,4096,128]{2,1,0:T(8,128)(2,1)}) %all-gather.5.cloned.1.call-update) | async-done | bytes 1048592 | tf_op jit(solution)/shard_map/all_gather | solution.py:159
  65.5 81.5 %all-gather.3.cloned.1.call-done = bf16[1,4096,512]{1,2,0:T(8,128)(2,1)} async-done(((bf16[1,256,512]{1,2,0:T(8,128)(2,1)}), bf16[1,4096,512]{1,2,0:T(8,128)(2,1)}) %all-gather.3.cloned.1.call-update) | async-done | bytes 4194320 | tf_op jit(solution)/shard_map/all_gather | solution.py:158
  147.1 9.1 %while.19 = (s32[]{:T(128)}, f32[1,14,256]{2,1,0:T(8,128)S(1)}, f32[1,14,256]{2,1,0:T(8,128)S(1)}, f32[1,14,256]{2,1,0:T(8,128)S(1)}, f32[1,7,256]{2,1,0:T(8,128...) while((s32[]{:T(128)}, f32[1,14,256]{2,1,0:T(8,128)S(1)}, ...), condition=%wide.region_6.7_spmd.clone, body=%wide.region_0.6_spmd.clone.sunk | while | flops 732774400 | bytes 37899856 | solution.py:102
  147.1 1.1 constant_dynamic-slice_fusion.3
  148.2 0.3 copy.33
  148.5 0.9 gather_fusion
  149.4 0.1 broadcast_compare_fusion.2
  149.6 1.4 fusion.28
  151.0 0.9 dynamic-slice_bitcast_fusion.2
  152.0 0.8 select_reduce_fusion.4
  152.8 2.6 fusion.29
  155.4 0.8 select_reduce_fusion.5
  156.3 0.1 fusion.23
  156.6 10.3 %psum.28 = f32[7]{0:T(128)S(1)} all-reduce(f32[7]{0:T(128)S(1)} %reduce_sum.64), channel_id=1, replica_groups=mesh['dp_0'=4,'dp_1'=2,'head'=2,'kv_0'=4,'kv_1'=4] {'dp_0'}, use_global_device_ids=true, to_apply=%region_10.11 | all-reduce | flops 7 | bytes 56 | tf_op jit(solution)/shard_map/psum | solution.py:39
  166.9 2.5 psum.29
  169.4 65.0 %psum.30 = f32[7]{0:T(128)S(1)} all-reduce(f32[7]{0:T(128)S(1)} %psum.29), channel_id=1, replica_groups=mesh['dp_0'=4,'dp_1'=2,'head'=2,'kv_0'=4,'kv_1'=4] {'kv_0'}, use_global_device_ids=true, to_apply=%region_12.13 | all-reduce | flops 7 | bytes 56 | tf_op jit(solution)/shard_map/psum | solution.py:39
  234.4 0.6 reduce_sum.61
  235.0 20.8 %psum.31 = f32[7]{0:T(128)S(1)} all-reduce(f32[7]{0:T(128)S(1)} %psum.30), channel_id=1, replica_groups=mesh['dp_0'=4,'dp_1'=2,'head'=2,'kv_0'=4,'kv_1'=4] {'kv_1'}, use_global_device_ids=true, to_apply=%region_13.14 | all-reduce | flops 7 | bytes 56 | tf_op jit(solution)/shard_map/psum | solution.py:39
  255.8 0.5 broadcast_multiply_fusion
  (43 shorter events, 0.9 us)
Async XLA Ops:
  7.2 19.2 %copy-start = (s32[14,2]{0,1:T(2,128)S(1)}, s32[14,2]{0,1:T(2,128)}, u32[]{:S(2)}) copy-start(s32[14,2]{0,1:T(2,128)} %param.11) | copy-start | bytes 340
  7.2 58.3 %all-gather.5.cloned.1.call-start = ((), (), s32[]{:S(2)}) async-start(), calls=%async_computation.3 | async-start | bytes 1114112 | tf_op jit(solution)/shard_map/all_gather | solution.py:159
  7.9 139.1 %all-gather.3.cloned.1.call-start = ((), (), s32[]{:S(2)}) async-start(), calls=%async_computation.2 | async-start | bytes 4456448 | tf_op jit(solution)/shard_map/all_gather | solution.py:158
  18.7 8.7 %copy-start.1 = (bf16[1,256,896]{2,1,0:T(8,128)(2,1)S(1)}, bf16[1,256,896]{2,1,0:T(8,128)(2,1)}, u32[]{:S(2)}) copy-start(bf16[1,256,896]{2,1,0:T(8,128)(2,1)} %param.9) | copy-start | bytes 1376260
  20.1 25.4 %all-to-all-start.1 = ((bf16[2,1,256,1792]{2,3,1,0:T(8,128)(2,1)}), bf16[2,1,256,1792]{2,3,1,0:T(8,128)(2,1)S(1)}, u32[]{:S(2)}, u32[]{:S(2)}) async-start(bf16[2,1,256,1792]{2,3,1,0:T(8,128)(2,1)} %broadcast_in_dim.101), calls=%async_computation.1 | async-start | bytes 3670016 | tf_op jit(solution)/shard_map/all_to_all | solution.py:21
  149.6 2.4 copy-start.2
Sparse Core Ops, SparseCore 0:
  10.4 55.0 all-gather.4
  67.9 79.0 all-gather.2
where the time goes:
time: 264 us; the launch traced here: 263 us
  waiting for transfers between devices  114 us (43%)
  blocking collectives  107 us (41%)
  between operations  16.8 us (6%)
  local copies, waits for them, and re-layouts  14.7 us (6%)
  other arithmetic  4.56 us (2%)
  starting transfers between devices  3.79 us (1%)
    psum x4, blocking collectives, one_axis_at_a_time(): shard = lax.psum(shard, axis)  98.5 us
    all_gather x1, waiting for transfers between devices, per_device(): lax.all_gather(all_tk, KV, axis=1, tiled=True)  81.5 us
    all_to_all x1, waiting for transfers between devices, from_everyone(): lax.all_to_all(jnp.broadcast_to(shard[None], (count, *shard.shape)), axis...  16.9 us
    all_gather x1, waiting for transfers between devices, per_device(): lax.all_gather(student_key, KV, axis=1, tiled=True)  15 us
    all_to_all x1, blocking collectives, from_everyone(): lax.all_to_all(jnp.broadcast_to(shard[None], (count, *shard.shape)), axis...  8.25 us
  transfers between devices with their start and end apart: 3, of which 3 were waited for; matrix products, arithmetic and copies ran while one was open for 4% of the time, Pallas kernels for 0%

commit v1 on v0

--- a/solution.py
+++ b/solution.py
@@ -4,6 +4,7 @@
 from jax import lax
 from jax.sharding import Mesh
 from jax.sharding import PartitionSpec as P
+from jax.lax import all_to_all, psum
 
 HT = 28
 KVT = 4
@@ -156,7 +157,10 @@
         initial,
         (
             lax.all_gather(all_tk, KV, axis=1, tiled=True),
-            lax.all_gather(student_key, KV, axis=1, tiled=True),
+            jnp.concatenate(
+                all_to_all(jnp.stack([student_key for _ in range(psum(1, KV))], axis=0), KV, 0, 0),
+                1,
+            ),
         ),
         jnp.int32(0),
     )

time: 264 us -> 245 us (0.928)
  waiting for transfers between devices: 114 us -> 47.4 us
  blocking collectives: 107 us -> 140 us
  starting transfers between devices: 3.79 us -> 14.2 us
    all_gather x1, waiting for transfers between devices: 81.5 us -> 17.4 us  [per_device(): lax.all_gather(all_tk, KV, axis=1, tiled=True)]
    all_to_all x1 -> x2, blocking collectives: 8.25 us -> 36 us  [from_everyone(): lax.all_to_all(jnp.broadcast_to(shard[None], (count, *shard.shape)), axis...]
    all_gather x1 -> x0, waiting for transfers between devices: 15 us -> none  [per_device(): lax.all_gather(student_key, KV, axis=1, tiled=True)]
    all_to_all x1, waiting for transfers between devices: 16.9 us -> 30 us  [per_device(): all_to_all(jnp.stack([student_key for _ in range(psum(1, KV))], axis=0),...]
    all_to_all x1, starting transfers between devices: 3.72 us -> 14.2 us  [per_device(): all_to_all(jnp.stack([student_key for _ in range(psum(1, KV))], axis=0),...]
    psum x4, blocking collectives: 98.5 us -> 104 us  [one_axis_at_a_time(): shard = lax.psum(shard, axis)]
  transfers between devices with their start and end apart: 3 -> 2, of which waited for: 3 -> 2; matrix products, arithmetic and copies ran while one was open for 4% -> 5% of each run, Pallas kernels for 0% -> 0%
where the time goes in v1:
time: 245 us; the launch traced here: 243 us
  blocking collectives  140 us (57%)
  waiting for transfers between devices  47.4 us (19%)
  between operations  16.8 us (7%)
  local copies, waits for them, and re-layouts  14.8 us (6%)
  starting transfers between devices  14.2 us (6%)
  other arithmetic  5.5 us (2%)
  matrix products  3.43 us (1%)
    psum x4, blocking collectives, one_axis_at_a_time(): shard = lax.psum(shard, axis)  104 us
    all_to_all x2, blocking collectives, from_everyone(): lax.all_to_all(jnp.broadcast_to(shard[None], (count, *shard.shape)), axis...  36 us
    all_to_all x1, waiting for transfers between devices, per_device(): all_to_all(jnp.stack([student_key for _ in range(psum(1, KV))], axis=0),...  30 us
    all_gather x1, waiting for transfers between devices, per_device(): lax.all_gather(all_tk, KV, axis=1, tiled=True)  17.4 us
    all_to_all x1, starting transfers between devices, per_device(): all_to_all(jnp.stack([student_key for _ in range(psum(1, KV))], axis=0),...  14.2 us
  transfers between devices with their start and end apart: 2, of which 2 were waited for; matrix products, arithmetic and copies ran while one was open for 5% of the time, Pallas kernels for 0%

profile of v1, /device:TPU:0, one launch (start us, length us, event | category | flops | bytes accessed | tf_op | source)
XLA Modules:
  0.0 242.5 jit_solution(11975710500207430732)
XLA Ops:
  7.2 1.0 copy.25
  8.3 8.2 %all_to_all.15 = bf16[2,1,256,256]{2,3,1,0:T(8,128)(2,1)} all-to-all(bf16[2,1,256,256]{2,3,1,0:T(8,128)(2,1)S(1)} %broadcast_in_dim.98), channel_id=1, replica_groups=mesh['dp_0'=4,'dp_1'=2,'head'=2,'kv_0'=4,'kv_1'=4] {'head'}, dimensions={0} | all-to-all | bytes 524288 | tf_op jit(solution)/shard_map/all_to_all | solution.py:22
  16.5 1.5 copy.26
  18.0 0.1 broadcast_in_dim.101
  18.1 27.8 %all_to_all.16 = bf16[2,1,256,1792]{2,3,1,0:T(8,128)(2,1)S(1)} all-to-all(bf16[2,1,256,1792]{2,3,1,0:T(8,128)(2,1)S(1)} %broadcast_in_dim.101), channel_id=1, replica_groups=mesh['dp_0'=4,'dp_1'=2,'head'=2,'kv_0'=4,'kv_1'=4] {'head'}, dimensions={0} | all-to-all | bytes 3670016 | tf_op jit(solution)/shard_map/all_to_all | solution.py:22
  45.9 1.2 stack.2
  47.1 14.2 %all-to-all-start.2 = ((bf16[16,1,256,128]{3,2,1,0:T(8,128)(2,1)}), bf16[16,1,256,128]{3,2,1,0:T(8,128)(2,1)S(1)}, u32[]{:S(2)}, u32[]{:S(2)}) async-start(bf16[16,1,256,128]{3,2,1,0:T(8,128)(2,1)} %stack.2), calls=%async_computation.2 | async-start | bytes 2097152 | tf_op jit(solution)/shard_map/all_to_all | solution.py:161
  61.3 0.6 slice.3
  64.9 1.2 copy.30
  66.1 1.0 copy.31
  67.1 2.6 %copy.29 = bf16[256,28,128]{2,0,1:T(8,128)(2,1)} copy(bf16[256,28,128]{0,2,1:T(8,128)(2,1)S(1)} %bitcast.108) | data formatting | bytes 3670016 | tf_op jit(solution)/shard_map/reshape;reshape | solution.py:148
  69.7 2.2 gather_fusion.1
  72.0 1.1 bitcast_select_fusion.1
  73.1 30.0 %all-to-all-done.2 = bf16[16,1,256,128]{3,2,1,0:T(8,128)(2,1)S(1)} async-done(((bf16[16,1,256,128]{3,2,1,0:T(8,128)(2,1)}), bf16[16,1,256,128]{3,2,1,0:T(8,128)(2,1)S(1)}, u32[]{:S(2)}, u32[]{:S(2)}) %all-to-all-start.2) | async-done | bytes 1048608 | tf_op jit(solution)/shard_map/all_to_all | solution.py:161
  103.0 17.4 %all-gather.2.cloned.1.call-done = bf16[1,4096,512]{1,2,0:T(8,128)(2,1)} async-done(((bf16[1,256,512]{1,2,0:T(8,128)(2,1)}), bf16[1,4096,512]{1,2,0:T(8,128)(2,1)}) %all-gather.2.cloned.1.call-update) | async-done | bytes 4194320 | tf_op jit(solution)/shard_map/all_gather | solution.py:159
  120.5 9.5 %while.19 = (s32[]{:T(128)}, f32[1,14,256]{2,1,0:T(8,128)S(1)}, f32[1,14,256]{2,1,0:T(8,128)S(1)}, f32[1,14,256]{2,1,0:T(8,128)S(1)}, f32[1,7,256]{2,1,0:T(8,128...) while((s32[]{:T(128)}, f32[1,14,256]{2,1,0:T(8,128)S(1)}, ...), condition=%wide.region_6.7_spmd.clone, body=%wide.region_0.6_spmd.clone.sunk | while | flops 732774400 | bytes 37899856 | solution.py:103
  120.5 1.1 constant_dynamic-slice_fusion.3
  121.6 0.3 copy.33
  121.9 0.9 gather_fusion
  122.8 0.1 broadcast_compare_fusion.2
  123.0 2.6 %fusion.28 = (f32[14,256]{1,0:T(8,128)S(1)}, f32[14,512,256]{2,1,0:T(8,128)S(1)}) fusion(pred[256,512]{0,1:T(8,128)(4,1)S(1)} %broadcast_compare_fusion.2, bf16[1,256,14,128]{3,1,2,0:T(8,128)(2,1)} %get-tuple-element.361, bf16[14,512,128]{2,1,0:T(8,128)(2,1)S(1)} %gather_fusion, pred[14]{0:T(512)(128)(4,1)S(1)} %compare_and_fusion.5), kind=kOutput, calls=%fused_computation.9.clone.1 | convolution fusion | flops 476180992 | bytes 10237966 | tf_op jit(solution)/shard_map/while/body/bqpd,bkpd->bpqk/dot_general | solution.py:77
  125.7 0.8 select_reduce_fusion.4
  126.5 2.6 %fusion.29 = (f32[14,256]{1,0:T(8,128)S(1)}, f32[14,256]{1,0:T(8,128)S(1)}) fusion(f32[14,512,256]{2,1,0:T(8,128)S(1)} %get-tuple-element.307, f32[7,256,512]{1,2,0:T(8,128)S(1)} %get-tuple-element.308, f32[14,256]{1,0:T(8,128)S(1)} %bitcast.109, pred[256,512]{0,1:T(8,128)(4,1)S(1)} %broadcast_compare_fusion.2), kind=kLoop, calls=%fused_computation.6.clone.1 | loop fusion | flops 14672896 | bytes 11184128 | tf_op jit(solution)/shard_map/while/body/reduce_sum | solution.py:100
  129.2 0.8 select_reduce_fusion.5
  130.0 0.1 fusion.23
  130.2 0.1 reduce_sum.64
  130.4 10.5 %psum.28 = f32[7]{0:T(128)S(1)} all-reduce(f32[7]{0:T(128)S(1)} %reduce_sum.64), channel_id=1, replica_groups=mesh['dp_0'=4,'dp_1'=2,'head'=2,'kv_0'=4,'kv_1'=4] {'dp_0'}, use_global_device_ids=true, to_apply=%region_10.11 | all-reduce | flops 7 | bytes 56 | tf_op jit(solution)/shard_map/psum | solution.py:40
  140.9 2.5 %psum.29 = f32[7]{0:T(128)S(1)} all-reduce(f32[7]{0:T(128)S(1)} %psum.28), channel_id=1, replica_groups=mesh['dp_0'=4,'dp_1'=2,'head'=2,'kv_0'=4,'kv_1'=4] {'dp_1'}, use_global_device_ids=true, to_apply=%region_11.12 | all-reduce | flops 7 | bytes 56 | tf_op jit(solution)/shard_map/psum | solution.py:40
  143.3 72.3 %psum.30 = f32[7]{0:T(128)S(1)} all-reduce(f32[7]{0:T(128)S(1)} %psum.29), channel_id=1, replica_groups=mesh['dp_0'=4,'dp_1'=2,'head'=2,'kv_0'=4,'kv_1'=4] {'kv_0'}, use_global_device_ids=true, to_apply=%region_12.13 | all-reduce | flops 7 | bytes 56 | tf_op jit(solution)/shard_map/psum | solution.py:40
  215.7 0.6 reduce_sum.61
  216.3 18.9 %psum.31 = f32[7]{0:T(128)S(1)} all-reduce(f32[7]{0:T(128)S(1)} %psum.30), channel_id=1, replica_groups=mesh['dp_0'=4,'dp_1'=2,'head'=2,'kv_0'=4,'kv_1'=4] {'kv_1'}, use_global_device_ids=true, to_apply=%region_13.14 | all-reduce | flops 7 | bytes 56 | tf_op jit(solution)/shard_map/psum | solution.py:40
  235.2 0.5 broadcast_multiply_fusion
  (42 shorter events, 0.7 us)
Async XLA Ops:
  7.2 56.7 %copy-start = (s32[14,2]{0,1:T(2,128)S(1)}, s32[14,2]{0,1:T(2,128)}, u32[]{:S(2)}) copy-start(s32[14,2]{0,1:T(2,128)} %param.11) | copy-start | bytes 340
  7.2 113.3 %all-gather.2.cloned.1.call-start = ((), (), s32[]{:S(2)}) async-start(), calls=%async_computation.3 | async-start | bytes 4456448 | tf_op jit(solution)/shard_map/all_gather | solution.py:159
  18.0 27.9 %copy-start.2 = (bf16[1,256,128]{2,1,0:T(8,128)(2,1)S(1)}, bf16[1,256,128]{2,1,0:T(8,128)(2,1)}, u32[]{:S(2)}) copy-start(bf16[1,256,128]{2,1,0:T(8,128)(2,1)} %param.10) | copy-start | bytes 196612
  47.1 55.9 %all-to-all-start.2 = ((bf16[16,1,256,128]{3,2,1,0:T(8,128)(2,1)}), bf16[16,1,256,128]{3,2,1,0:T(8,128)(2,1)S(1)}, u32[]{:S(2)}, u32[]{:S(2)}) async-start(bf16[16,1,256,128]{3,2,1,0:T(8,128)(2,1)} %stack.2), calls=%async_computation.2 | async-start | bytes 2097152 | tf_op jit(solution)/shard_map/all_to_all | solution.py:161
  123.0 2.7 %copy-start.1 = (bf16[1,256,7,128]{3,1,2,0:T(8,128)(2,1)S(1)}, bf16[1,256,7,128]{3,1,2,0:T(8,128)(2,1)}, u32[]{:S(2)}) copy-start(bf16[1,256,7,128]{3,1,2,0:T(8,128)(2,1)} %get-tuple-element.363) | copy-start | bytes 1376260 | tf_op jit(solution)/shard_map/while
Sparse Core Ops, SparseCore 0:
  16.7 103.7 all-gather.1
